TPU v7x, 32 devices: a whole 2x2x4 slice. The times are simulated.
32 devices in a mesh: row: 16 (over z, x, core), col: 2 (over y).
Axes of the slice: x: 2, y: 2, z: 4, core: 2. Of those that a mesh axis runs over, the one named last changes fastest.
Arguments:
- species: float32 [2, 128, 128, 64], P(None, None, 'row', 'col'), may hold values from -6 to 6
- symbol_x: float32 [128], replicated, may hold values from 0.3 to 3
- symbol_y: float32 [128], replicated, may hold values from 0.3 to 3
- symbol_z: float32 [64], replicated, may hold values from 0.3 to 3
Outputs:
- spectrum: float32 [2, 128, 128, 64], P(None, 'row', 'col')
All inputs are finite; a program needn't handle non-finite values.
Results may differ from a plain program's by a relative error of at most 0.00007.
Values sent between devices are 32-bit elements; how exact they have to be, the bound alone decides.
A program may use at most 64 MiB of HBM per device.

v0:
```python
import functools

import jax
import jax.numpy as jnp
import ml_dtypes
import numpy as np
from jax import lax
from jax.experimental import pallas as pl
from jax.experimental.pallas import tpu as pltpu
from jax.sharding import PartitionSpec as P

LANES = 128
CUTS = 1
F32, BF16 = jnp.float32, jnp.bfloat16


def basis_table(count):
    odd = 2 * np.arange(count) + 1
    angle = np.pi / (4 * count) * (odd[:, None] * odd[None, :] % (8 * count))
    return np.cos(angle) * (2.0 / count) ** 0.5


def halves(table):
    high = table.astype(ml_dtypes.bfloat16)
    low = (table - high.astype(np.float64)).astype(ml_dtypes.bfloat16)
    return high, low


def split(values):
    high = values.astype(BF16)
    low = (values - high.astype(F32)).astype(BF16)
    return high, low


def tables(nx, ny, nz, share_z):
    width = LANES // share_z
    lane = np.arange(nx)
    group, rest = lane // LANES, lane % LANES
    order = width * (group * share_z + rest % share_z) + rest // share_z
    high, low = halves(basis_table(nx)[:, order])
    table_x = np.block([[high, low], [high, low]])
    high, low = halves(basis_table(ny))
    table_y = np.block([[high, high], [low, low]])
    eye = np.eye(width)
    wide = np.concatenate(
        [np.kron(eye, part) for part in np.split(basis_table(nz), nz // share_z, axis=0)], axis=0
    )
    table_z = np.stack(halves(wide))
    return table_x, table_y, table_z


def kernel(
    rows, cols, names,
    species, hx_hbm, hy_hbm, sx_hbm, sy_hbm, sz_hbm,
    lines, scale,
    xin, hx, hy, sx, sy, sz, send, recv, mixed, tall_x, tall_y,
    in_sem, row_send, row_recv, col_send, col_recv,
):
    row_name, col_name = names
    fields, share_y, share_z, nx = species.shape
    ny = rows * share_y
    nz = sz.shape[1]
    share_x, half_y = nx // rows, ny // cols
    width = LANES // share_z
    quads = share_x // width
    wide = quads * LANES // CUTS
    me, my_col = lax.axis_index(row_name), lax.axis_index(col_name)

    barrier = pltpu.get_barrier_semaphore()
    for k in range(1, rows):
        pl.semaphore_signal(
            barrier, inc=1, device_id={row_name: (me + k) % rows},
            device_id_type=pl.DeviceIdType.MESH,
        )
    for k in range(1, cols):
        pl.semaphore_signal(
            barrier, inc=1, device_id={col_name: (my_col + k) % cols},
            device_id_type=pl.DeviceIdType.MESH,
        )

    loads = [pltpu.make_async_copy(species.at[f], xin.at[f], in_sem.at[f]) for f in range(fields)]
    pairs = ((hx_hbm, hx), (hy_hbm, hy), (sx_hbm, sx), (sy_hbm, sy), (sz_hbm, sz))
    fetches = [
        pltpu.make_async_copy(a, b, in_sem.at[fields + i]) for i, (a, b) in enumerate(pairs)
    ]
    loads[0].start()
    fetches[0].start()
    for copy in loads[1:] + fetches[1:]:
        copy.start()

    lane = lax.broadcasted_iota(jnp.int32, (share_y, LANES), 1)
    order = sorted(range(1, rows), key=lambda k: -min(k, rows - k))

    def row_copy(piece, target, origin):
        return pltpu.make_async_remote_copy(
            src_ref=send.at[piece, target],
            dst_ref=recv.at[piece, origin],
            send_sem=row_send.at[piece, target],
            recv_sem=row_recv.at[piece, origin],
            device_id={row_name: target},
            device_id_type=pl.DeviceIdType.MESH,
        )

    def col_copy(piece, target, origin):
        return pltpu.make_async_remote_copy(
            src_ref=mixed.at[piece, target],
            dst_ref=lines.at[piece, origin],
            send_sem=col_send.at[piece, target],
            recv_sem=col_recv.at[piece, origin],
            device_id={col_name: target},
            device_id_type=pl.DeviceIdType.MESH,
        )

    for f in range(fields):
        loads[f].wait()
        if f == 0:
            fetches[0].wait()
        high, low = split(
            jnp.concatenate(
                [xin[f, :, z, :] for z in range(share_z)], axis=0
            )
        )
        both = jnp.dot(
            jnp.concatenate([high, low], axis=1), hx[...], preferred_element_type=F32
        )
        both = both[:, :nx] + both[:, nx:]
        for group in range(nx // LANES):
            tiles = [
                both[z * share_y : (z + 1) * share_y, group * LANES : (group + 1) * LANES]
                for z in range(share_z)
            ]
            bit = 1
            while bit < share_z:
                keep = (lane & bit) == 0
                for i in range(share_z):
                    if i & bit == 0:
                        a, b = tiles[i], tiles[i + bit]
                        tiles[i] = jnp.where(keep, a, pltpu.roll(b, bit, 1))
                        tiles[i + bit] = jnp.where(keep, pltpu.roll(a, LANES - bit, 1), b)
                bit *= 2
            for i in range(share_z):
                q = group * share_z + i
                target, at = q // quads, q % quads * LANES
                send[f * CUTS + at // wide, target, :, at % wide : at % wide + LANES] = tiles[i]
        if f == 0:
            pl.semaphore_wait(barrier, rows + cols - 2)
        for cut in range(CUTS):
            piece = f * CUTS + cut
            for k in order:
                row_copy(piece, (me + k) % rows, me).start()
            recv[piece, me] = send[piece, me]

    for copy in fetches[1:]:
        copy.wait()
    tall_x[...] = jnp.broadcast_to(sx[...], (LANES, nx)).T
    tall_y[...] = jnp.broadcast_to(sy[...], (LANES, ny)).T
    part_y = tall_y[pl.ds(my_col * half_y, half_y), :1]
    for x in range(share_x):
        part_x = tall_x[pl.ds(me * share_x + x, 1), :1]
        at = x % width * nz
        scale[x // width, :, at : at + nz] = 1.0 / (part_x + part_y + sz[...])

    for piece in range(fields * CUTS):
        for k in order:
            origin = (me + rows - k) % rows
            row_copy(piece, origin, origin).wait_recv()
        high, low = split(recv[piece].reshape(ny, wide))
        both = jnp.dot(
            hy[...], jnp.concatenate([high, low], axis=0), preferred_element_type=F32
        )
        both = both[:ny] + both[ny:]
        mixed[piece] = both.reshape(cols, half_y, wide)
        for k in range(1, cols):
            col_copy(piece, (my_col + k) % cols, my_col).start()
        lines[piece, my_col] = mixed[piece, my_col]

    for piece in range(fields * CUTS):
        for k in order:
            row_copy(piece, (me + k) % rows, me).wait_send()
        for k in range(1, cols):
            origin = (my_col + cols - k) % cols
            col_copy(piece, origin, origin).wait_recv()
            col_copy(piece, (my_col + k) % cols, my_col).wait_send()


def last_kernel(lines, scale, wz, out, held, out_sem):
    pieces, cols, half_y, wide = lines.shape
    nz = out.shape[3]
    width = scale.shape[2] // nz
    copies = []
    for piece in range(pieces):
        f, cut = piece // CUTS, piece % CUTS
        for i in range(wide // LANES):
            quad = cut * (wide // LANES) + i
            line = jnp.concatenate(
                [lines[piece, c, :, i * LANES : (i + 1) * LANES] for c in range(cols)], axis=1
            )
            high, low = split(line)
            both = jnp.dot(
                jnp.concatenate([high, low], axis=0), wz[0], preferred_element_type=F32
            )
            done = both[:half_y] + both[half_y:]
            done = done + jnp.dot(high, wz[1], preferred_element_type=F32)
            done = done * scale[quad]
            for j in range(width):
                held[f, quad * width + j] = done[:, j * nz : (j + 1) * nz]
            span = pl.ds(quad * width, width)
            copy = pltpu.make_async_copy(held.at[f, span], out.at[f, span], out_sem.at[f, quad])
            copy.start()
            copies.append(copy)
    for copy in copies:
        copy.wait()


def on_device(rows, cols, species, symbol_x, symbol_y, symbol_z):
    fields, nx, share_y, share_z = species.shape
    ny, nz = symbol_y.shape[0], symbol_z.shape[0]
    share_x, half_y = nx // rows, ny // cols
    width = LANES // share_z
    pieces, wide = fields * CUTS, share_x // width * LANES // CUTS
    hx, hy, wz = (jnp.asarray(t) for t in tables(nx, ny, nz, share_z))
    dma = pltpu.SemaphoreType.DMA
    width_z = width * nz
    vmem = pl.BlockSpec(memory_space=pltpu.VMEM)
    lines, scale = pl.pallas_call(
        functools.partial(kernel, rows, cols, ("row", "col")),
        out_shape=(
            jax.ShapeDtypeStruct((pieces, cols, half_y, wide), F32),
            jax.ShapeDtypeStruct((share_x // width, half_y, width_z), F32),
        ),
        in_specs=[pl.BlockSpec(memory_space=pl.ANY)] * 6,
        out_specs=(vmem, vmem),
        scratch_shapes=[
            pltpu.VMEM((fields, share_y, share_z, nx), F32),
            pltpu.VMEM(hx.shape, BF16),
            pltpu.VMEM(hy.shape, BF16),
            pltpu.VMEM((1, nx), F32),
            pltpu.VMEM((1, ny), F32),
            pltpu.VMEM((1, nz), F32),
            pltpu.VMEM((pieces, rows, share_y, wide), F32),
            pltpu.VMEM((pieces, rows, share_y, wide), F32),
            pltpu.VMEM((pieces, cols, half_y, wide), F32),
            pltpu.VMEM((nx, LANES), F32),
            pltpu.VMEM((ny, LANES), F32),
            dma((fields + 5,)),
            dma((pieces, rows)),
            dma((pieces, rows)),
            dma((pieces, cols)),
            dma((pieces, cols)),
        ],
        compiler_params=pltpu.CompilerParams(collective_id=0, has_side_effects=True, vmem_limit_bytes=16 * 2**20),
    )(
        *(pltpu.with_memory_space_constraint(v, pltpu.HBM) for v in (jnp.transpose(species, (0, 2, 3, 1)), hx, hy,
        symbol_x[None, :], symbol_y[None, :], symbol_z[None, :])),
    )
    shape = (fields, share_x, half_y, nz)
    return pl.pallas_call(
        last_kernel,
        out_shape=jax.ShapeDtypeStruct(shape, F32),
        in_specs=[vmem, vmem, vmem],
        out_specs=pl.BlockSpec(memory_space=pl.ANY),
        scratch_shapes=[pltpu.VMEM(shape, F32), dma((fields, share_x // width))],
        compiler_params=pltpu.CompilerParams(vmem_limit_bytes=16 * 2**20),
    )(lines, scale, wz)


def solution(mesh):
    rows, cols = mesh.shape["row"], mesh.shape["col"]
    in_specs = (P(None, None, "row", "col"), P(), P(), P())
    out_specs = P(None, "row", "col", None)
    return jax.shard_map(
        functools.partial(on_device, rows, cols),
        mesh=mesh, in_specs=in_specs, out_specs=out_specs, check_vma=False,
    )
```

profile of v0, /device:TPU:0, one launch (start us, length us, event | category | flops | bytes accessed | tf_op | source)
XLA Modules:
  0.0 18.7 jit_solution(13972454074693541848)
XLA Ops:
  0.0 0.0 copy-start
  0.0 17.6 %shard_map.73 = (f32[2,2,64,256]{3,2,1,0:T(8,128)S(1)}, f32[2,64,256]{2,1,0:T(8,128)S(1)}) custom-call(f32[2,8,32,128]{3,2,1,0:T(8,128)} %bitcast.4, bf16[256,256]{1,0:T(8,128)(2,1)} %constant.6.clone.hx_hbm, bf16[256,256]{1,0:T(8,128)(2,1)} %constant.7.clone.hy_hbm, f32[1,128]{1,0:T(1,128)} %bitcast.5, f32[1,128]{1,0:T(1,128)} %bitcast.6, f32[1,64]{1,0:T(1,128)} %bitcast.7), custom_call_target="tpu_custom_call" | custom-call | tf_op jit(solution)/shard_map/pallas_call | solution.py:225
  17.6 0.0 copy-done
  17.6 1.1 %shard_map.74 = f32[2,8,64,64]{3,2,1,0:T(8,128)} custom-call(f32[2,2,64,256]{3,2,1,0:T(8,128)S(1)} %get-tuple-element.7.lines, f32[2,64,256]{2,1,0:T(8,128)S(1)} %get-tuple-element.8.scale, bf16[2,256,256]{2,1,0:T(8,128)(2,1)S(1)} %copy-done), custom_call_target="tpu_custom_call" | custom-call | tf_op jit(solution)/shard_map/pallas_call | solution.py:257
Async XLA Ops:
  0.0 17.6 %copy-start = (bf16[2,256,256]{2,1,0:T(8,128)(2,1)S(1)}, bf16[2,256,256]{2,1,0:T(8,128)(2,1)}, u32[]{:S(2)}) copy-start(bf16[2,256,256]{2,1,0:T(8,128)(2,1)} %constant.8.clone.wz) | copy-start | bytes 786436
where the time goes:
time: 18.9 us; the launch traced here: 18.7 us
  Pallas kernels  18.7 us (99%)
    pallas_call x1, Pallas kernels, on_device(): pl.pallas_call(functools.partial(kernel, rows, cols, ('row', 'col')), out...  17.6 us
    pallas_call x1, Pallas kernels, on_device(): pl.pallas_call(last_kernel, out_shape=jax.ShapeDtypeStruct(shape, F32), i...  1.14 us

commit v1 on v0

--- a/solution.py
+++ b/solution.py
@@ -10,8 +10,10 @@
 from jax.sharding import PartitionSpec as P
 
 LANES = 128
-CUTS = 1
+CUTS = 2
+GROUP = 4
 F32, BF16 = jnp.float32, jnp.bfloat16
+MESH = pl.DeviceIdType.MESH
 
 
 def basis_table(count):
@@ -54,7 +56,7 @@
     species, hx_hbm, hy_hbm, sx_hbm, sy_hbm, sz_hbm,
     lines, scale,
     xin, hx, hy, sx, sy, sz, send, recv, mixed, tall_x, tall_y,
-    in_sem, row_send, row_recv, col_send, col_recv,
+    in_sem, row_send, row_recv, col_send, col_recv, row_ready, col_ready,
 ):
     row_name, col_name = names
     fields, share_y, share_z, nx = species.shape
@@ -64,19 +66,9 @@
     width = LANES // share_z
     quads = share_x // width
     wide = quads * LANES // CUTS
+    pieces = fields * CUTS
+    groups = row_ready.shape[0]
     me, my_col = lax.axis_index(row_name), lax.axis_index(col_name)
-
-    barrier = pltpu.get_barrier_semaphore()
-    for k in range(1, rows):
-        pl.semaphore_signal(
-            barrier, inc=1, device_id={row_name: (me + k) % rows},
-            device_id_type=pl.DeviceIdType.MESH,
-        )
-    for k in range(1, cols):
-        pl.semaphore_signal(
-            barrier, inc=1, device_id={col_name: (my_col + k) % cols},
-            device_id_type=pl.DeviceIdType.MESH,
-        )
 
     loads = [pltpu.make_async_copy(species.at[f], xin.at[f], in_sem.at[f]) for f in range(fields)]
     pairs = ((hx_hbm, hx), (hy_hbm, hy), (sx_hbm, sx), (sy_hbm, sy), (sz_hbm, sz))
@@ -85,36 +77,89 @@
     ]
     loads[0].start()
     fetches[0].start()
-    for copy in loads[1:] + fetches[1:]:
+    for copy in loads[1:]:
         copy.start()
 
+    barrier = pltpu.get_barrier_semaphore()
+
+    def greet_row(t, carry):
+        pl.semaphore_signal(barrier, inc=1, device_id={row_name: t}, device_id_type=MESH)
+        return carry
+
+    def greet_col(t, carry):
+        pl.semaphore_signal(barrier, inc=1, device_id={col_name: t}, device_id_type=MESH)
+        return carry
+
+    lax.fori_loop(me + 1, rows, greet_row, 0)
+    lax.fori_loop(my_col + 1, cols, greet_col, 0)
+    for copy in fetches[1:]:
+        copy.start()
+
+    @pl.when(me + my_col > 0)
+    def _():
+        with jax.named_scope("barrier"):
+            pl.semaphore_wait(barrier, me + my_col)
+
+    def ready_row(t, carry):
+        pl.semaphore_signal(
+            row_ready.at[me // GROUP], inc=1, device_id={row_name: t}, device_id_type=MESH
+        )
+        return carry
+
+    def ready_col(t, carry):
+        pl.semaphore_signal(col_ready, inc=1, device_id={col_name: t}, device_id_type=MESH)
+        return carry
+
+    lax.fori_loop(0, me, ready_row, 0)
+    lax.fori_loop(0, my_col, ready_col, 0)
+
     lane = lax.broadcasted_iota(jnp.int32, (share_y, LANES), 1)
-    order = sorted(range(1, rows), key=lambda k: -min(k, rows - k))
-
-    def row_copy(piece, target, origin):
+
+    def row_copy(piece, target):
         return pltpu.make_async_remote_copy(
             src_ref=send.at[piece, target],
-            dst_ref=recv.at[piece, origin],
-            send_sem=row_send.at[piece, target],
-            recv_sem=row_recv.at[piece, origin],
+            dst_ref=recv.at[piece, me],
+            send_sem=row_send.at[piece],
+            recv_sem=row_recv.at[piece],
             device_id={row_name: target},
-            device_id_type=pl.DeviceIdType.MESH,
-        )
-
-    def col_copy(piece, target, origin):
+            device_id_type=MESH,
+        )
+
+    def row_all(piece):
+        return pltpu.make_async_remote_copy(
+            src_ref=send.at[piece, pl.ds(0, rows - 1)],
+            dst_ref=recv.at[piece, pl.ds(0, rows - 1)],
+            send_sem=row_send.at[piece],
+            recv_sem=row_recv.at[piece],
+            device_id={row_name: me},
+            device_id_type=MESH,
+        )
+
+    def col_copy(piece, target):
         return pltpu.make_async_remote_copy(
             src_ref=mixed.at[piece, target],
-            dst_ref=lines.at[piece, origin],
-            send_sem=col_send.at[piece, target],
-            recv_sem=col_recv.at[piece, origin],
+            dst_ref=lines.at[piece, my_col],
+            send_sem=col_send.at[piece],
+            recv_sem=col_recv.at[piece],
             device_id={col_name: target},
-            device_id_type=pl.DeviceIdType.MESH,
+            device_id_type=MESH,
+        )
+
+    def col_all(piece):
+        return pltpu.make_async_remote_copy(
+            src_ref=mixed.at[piece, pl.ds(0, cols - 1)],
+            dst_ref=lines.at[piece, pl.ds(0, cols - 1)],
+            send_sem=col_send.at[piece],
+            recv_sem=col_recv.at[piece],
+            device_id={col_name: my_col},
+            device_id_type=MESH,
         )
 
     for f in range(fields):
-        loads[f].wait()
-        if f == 0:
-            fetches[0].wait()
+        with jax.named_scope(f"load{f}"):
+            loads[f].wait()
+            if f == 0:
+                fetches[0].wait()
         high, low = split(
             jnp.concatenate(
                 [xin[f, :, z, :] for z in range(share_z)], axis=0
@@ -142,13 +187,32 @@
                 q = group * share_z + i
                 target, at = q // quads, q % quads * LANES
                 send[f * CUTS + at // wide, target, :, at % wide : at % wide + LANES] = tiles[i]
-        if f == 0:
-            pl.semaphore_wait(barrier, rows + cols - 2)
-        for cut in range(CUTS):
-            piece = f * CUTS + cut
-            for k in order:
-                row_copy(piece, (me + k) % rows, me).start()
-            recv[piece, me] = send[piece, me]
+        with jax.named_scope(f"lower{f}"):
+            for cut in range(CUTS):
+                piece = f * CUTS + cut
+
+                def send_lower(t, carry, piece=piece):
+                    row_copy(piece, t).start()
+                    return carry
+
+                lax.fori_loop(0, me, send_lower, 0)
+                recv[piece, me] = send[piece, me]
+
+    for g in range(groups):
+        least, most = g * GROUP, min(rows, (g + 1) * GROUP)
+        first = jnp.maximum(least, me + 1)
+
+        @pl.when(first < most)
+        def _():
+            with jax.named_scope(f"ready{g}"):
+                pl.semaphore_wait(row_ready.at[g], most - first)
+            for piece in range(pieces):
+
+                def send_higher(t, carry, piece=piece):
+                    row_copy(piece, t).start()
+                    return carry
+
+                lax.fori_loop(first, most, send_higher, 0)
 
     for copy in fetches[1:]:
         copy.wait()
@@ -160,10 +224,14 @@
         at = x % width * nz
         scale[x // width, :, at : at + nz] = 1.0 / (part_x + part_y + sz[...])
 
-    for piece in range(fields * CUTS):
-        for k in order:
-            origin = (me + rows - k) % rows
-            row_copy(piece, origin, origin).wait_recv()
+    @pl.when(my_col < cols - 1)
+    def _():
+        pl.semaphore_wait(col_ready, cols - 1 - my_col)
+
+
+    for piece in range(pieces):
+        with jax.named_scope(f"rowwait{piece}"):
+            row_all(piece).wait_recv()
         high, low = split(recv[piece].reshape(ny, wide))
         both = jnp.dot(
             hy[...], jnp.concatenate([high, low], axis=0), preferred_element_type=F32
@@ -171,16 +239,15 @@
         both = both[:ny] + both[ny:]
         mixed[piece] = both.reshape(cols, half_y, wide)
         for k in range(1, cols):
-            col_copy(piece, (my_col + k) % cols, my_col).start()
+            col_copy(piece, (my_col + k) % cols).start()
         lines[piece, my_col] = mixed[piece, my_col]
 
-    for piece in range(fields * CUTS):
-        for k in order:
-            row_copy(piece, (me + k) % rows, me).wait_send()
-        for k in range(1, cols):
-            origin = (my_col + cols - k) % cols
-            col_copy(piece, origin, origin).wait_recv()
-            col_copy(piece, (my_col + k) % cols, my_col).wait_send()
+    for piece in range(pieces):
+        with jax.named_scope(f"sendwait{piece}"):
+            row_all(piece).wait_send()
+        with jax.named_scope(f"colwait{piece}"):
+            col_all(piece).wait_send()
+            col_all(piece).wait_recv()
 
 
 def last_kernel(lines, scale, wz, out, held, out_sem):
@@ -208,8 +275,9 @@
             copy = pltpu.make_async_copy(held.at[f, span], out.at[f, span], out_sem.at[f, quad])
             copy.start()
             copies.append(copy)
-    for copy in copies:
-        copy.wait()
+    with jax.named_scope("outwait"):
+        for copy in copies:
+            copy.wait()
 
 
 def on_device(rows, cols, species, symbol_x, symbol_y, symbol_z):
@@ -220,6 +288,7 @@
     pieces, wide = fields * CUTS, share_x // width * LANES // CUTS
     hx, hy, wz = (jnp.asarray(t) for t in tables(nx, ny, nz, share_z))
     dma = pltpu.SemaphoreType.DMA
+    regular = pltpu.SemaphoreType.REGULAR
     width_z = width * nz
     vmem = pl.BlockSpec(memory_space=pltpu.VMEM)
     lines, scale = pl.pallas_call(
@@ -243,10 +312,12 @@
             pltpu.VMEM((nx, LANES), F32),
             pltpu.VMEM((ny, LANES), F32),
             dma((fields + 5,)),
-            dma((pieces, rows)),
-            dma((pieces, rows)),
-            dma((pieces, cols)),
-            dma((pieces, cols)),
+            dma((pieces,)),
+            dma((pieces,)),
+            dma((pieces,)),
+            dma((pieces,)),
+            regular((pl.cdiv(rows, GROUP),)),
+            regular,
         ],
         compiler_params=pltpu.CompilerParams(collective_id=0, has_side_effects=True, vmem_limit_bytes=16 * 2**20),
     )(

time: 18.9 us -> 18 us (0.952)
  Pallas kernels: 18.7 us -> 17.8 us
    pallas_call x1, Pallas kernels: 17.6 us -> 16.7 us  [on_device(): pl.pallas_call(functools.partial(kernel, rows, cols, ('row', 'col')), out...]
where the time goes in v1:
time: 18 us; the launch traced here: 17.8 us
  Pallas kernels  17.8 us (99%)
    pallas_call x1, Pallas kernels, on_device(): pl.pallas_call(functools.partial(kernel, rows, cols, ('row', 'col')), out...  16.7 us
    pallas_call x1, Pallas kernels, on_device(): pl.pallas_call(last_kernel, out_shape=jax.ShapeDtypeStruct(shape, F32), i...  1.14 us

profile of v1, /device:TPU:0, one launch (start us, length us, event | category | flops | bytes accessed | tf_op | source)
XLA Modules:
  0.0 17.8 jit_solution(11014813481974797128)
XLA Ops:
  0.0 0.0 copy-start
  0.0 16.7 %shard_map.73 = (f32[4,2,64,128]{3,2,1,0:T(8,128)S(1)}, f32[2,64,256]{2,1,0:T(8,128)S(1)}) custom-call(f32[2,8,32,128]{3,2,1,0:T(8,128)} %bitcast.4, bf16[256,256]{1,0:T(8,128)(2,1)} %constant.6.clone.hx_hbm, bf16[256,256]{1,0:T(8,128)(2,1)} %constant.7.clone.hy_hbm, f32[1,128]{1,0:T(1,128)} %bitcast.5, f32[1,128]{1,0:T(1,128)} %bitcast.6, f32[1,64]{1,0:T(1,128)} %bitcast.7), custom_call_target="tpu_custom_call" | custom-call | tf_op jit(solution)/shard_map/pallas_call | solution.py:294
  16.7 0.0 copy-done
  16.7 1.1 %shard_map.74 = f32[2,8,64,64]{3,2,1,0:T(8,128)} custom-call(f32[4,2,64,128]{3,2,1,0:T(8,128)S(1)} %get-tuple-element.7.lines, f32[2,64,256]{2,1,0:T(8,128)S(1)} %get-tuple-element.8.scale, bf16[2,256,256]{2,1,0:T(8,128)(2,1)S(1)} %copy-done), custom_call_target="tpu_custom_call" | custom-call | tf_op jit(solution)/shard_map/pallas_call | solution.py:328
Async XLA Ops:
  0.0 16.7 %copy-start = (bf16[2,256,256]{2,1,0:T(8,128)(2,1)S(1)}, bf16[2,256,256]{2,1,0:T(8,128)(2,1)}, u32[]{:S(2)}) copy-start(bf16[2,256,256]{2,1,0:T(8,128)(2,1)} %constant.8.clone.wz) | copy-start | bytes 786436

commit v2 on v1

v2 whole, which is shorter than its diff:
```python
import functools

import jax
import jax.numpy as jnp
import ml_dtypes
import numpy as np
from jax import lax
from jax.experimental import pallas as pl
from jax.experimental.pallas import tpu as pltpu
from jax.sharding import PartitionSpec as P

LANES = 128
GROUP = 4
F32, BF16 = jnp.float32, jnp.bfloat16
MESH = pl.DeviceIdType.MESH


def basis_table(count):
    odd = 2 * np.arange(count) + 1
    angle = np.pi / (4 * count) * (odd[:, None] * odd[None, :] % (8 * count))
    return np.cos(angle) * (2.0 / count) ** 0.5


def halves(table):
    high = table.astype(ml_dtypes.bfloat16)
    low = (table - high.astype(np.float64)).astype(ml_dtypes.bfloat16)
    return high, low


def split(values):
    high = values.astype(BF16)
    low = (values - high.astype(F32)).astype(BF16)
    return high, low


def padded(count):
    return -(-count // LANES) * LANES


def tables(rows, nx, ny, nz, share_z):
    width, half = LANES // share_z, share_z // 2
    share_x = nx // rows
    lane = np.arange(LANES)
    blocks = []
    for quad in range(share_x // width):
        for first in range(0, rows, half):
            column = lane[: LANES // 2]
            x = (first + column % half) * share_x + quad * width + column // half
            high, low = halves(basis_table(nx)[:, x])
            blocks += [high, low]
    table_x = np.tile(np.concatenate(blocks, axis=1), (2, 1))
    high, low = halves(basis_table(ny))
    table_y = np.block([[high, high], [low, low]])
    wide = np.zeros((nz // share_z, LANES, width, padded(nz)))
    for start in range(nz // share_z):
        z = start * share_z + lane % half + half * (lane // (LANES // 2))
        wide[start, lane, lane % (LANES // 2) // half, :nz] = basis_table(nz)[z]
    table_z = np.stack(halves(wide.reshape(-1, width * padded(nz))))
    return table_x, table_y, table_z


def kernel(
    rows, cols, names,
    species, hx_hbm, hy_hbm, wz_hbm, sx_hbm, sy_hbm, sz_hbm,
    lines, scale, early,
    xin, mid, hx, hy, wz, sx, sy, sz, send, recv, mixed, gathered, tall_x, tall_y,
    in_sem, row_send, row_recv, col_send, col_recv, row_ready, col_ready,
):
    row_name, col_name = names
    fields, _, _, nx = species.shape
    ny, nz = sy.shape[1], sz.shape[1]
    share_y, share_z = ny // rows, nz // cols
    share_x, half_y = nx // rows, ny // cols
    width, half = LANES // share_z, share_z // 2
    quads = share_x // width
    pieces = fields * quads
    groups = row_ready.shape[0]
    middle = groups // 2 - 1
    me, my_col = lax.axis_index(row_name), lax.axis_index(col_name)
    mine = me // GROUP

    def fetch(source, target, semaphore, parts):
        step = source.shape[0] // parts
        for i in range(parts):
            span = pl.ds(i * step, step)
            pltpu.make_async_copy(source.at[span], target.at[span], semaphore).start()

    blocks = nx // LANES
    fetch(hx_hbm, hx, in_sem.at[0], 4)
    for f in range(fields):
        for b in range(blocks):
            for y in range(share_y):
                pltpu.make_async_copy(
                    species.at[f, y, :, pl.ds(b * LANES, LANES)], xin.at[f, b, :, y, :], in_sem.at[1 + f]
                ).start()

    barrier = pltpu.get_barrier_semaphore()

    def greet_row(t, carry):
        pl.semaphore_signal(barrier, inc=1, device_id={row_name: t}, device_id_type=MESH)
        return carry

    def greet_col(t, carry):
        pl.semaphore_signal(barrier, inc=1, device_id={col_name: t}, device_id_type=MESH)
        return carry

    is_middle = mine == middle
    past = mine == middle + 1
    back = (mine - 1) * GROUP
    lax.fori_loop(jnp.where(past, back, 0), jnp.where(past, back + GROUP, 0), greet_row, 0)
    lax.fori_loop(me + 1, rows, greet_row, 0)
    lax.fori_loop(my_col + 1, cols, greet_col, 0)
    rest = ((hy_hbm, hy), (wz_hbm, wz), (sx_hbm, sx), (sy_hbm, sy), (sz_hbm, sz))
    fetches = [
        pltpu.make_async_copy(a, b, in_sem.at[1 + fields + i]) for i, (a, b) in enumerate(rest)
    ]
    for copy in fetches:
        copy.start()

    def ready_row(t, carry):
        pl.semaphore_signal(row_ready.at[mine], inc=1, device_id={row_name: t}, device_id_type=MESH)
        return carry

    def ready_col(t, carry):
        pl.semaphore_signal(col_ready, inc=1, device_id={col_name: t}, device_id_type=MESH)
        return carry

    def meet():
        count = me + my_col + jnp.where(is_middle, GROUP, 0)

        @pl.when(count > 0)
        def _():
            with jax.named_scope("barrier"):
                pl.semaphore_wait(barrier, count)

        lax.fori_loop(0, jnp.where(past, back, me), ready_row, 0)
        lax.fori_loop(jnp.where(past, mine * GROUP, me), me, ready_row, 0)
        lax.fori_loop(0, my_col, ready_col, 0)

    soon = (me % GROUP >= GROUP // 2) & ~is_middle
    pl.when(soon)(meet)

    lane = lax.broadcasted_iota(jnp.int32, (share_y, LANES), 1)

    def row_copy(piece, target):
        return pltpu.make_async_remote_copy(
            src_ref=send.at[piece, target],
            dst_ref=recv.at[piece, me],
            send_sem=row_send.at[piece],
            recv_sem=row_recv.at[piece],
            device_id={row_name: target},
            device_id_type=MESH,
        )

    def row_all(piece):
        return pltpu.make_async_remote_copy(
            src_ref=send.at[piece, pl.ds(0, rows - 1)],
            dst_ref=recv.at[piece, pl.ds(0, rows - 1)],
            send_sem=row_send.at[piece],
            recv_sem=row_recv.at[piece],
            device_id={row_name: me},
            device_id_type=MESH,
        )

    def col_copy(piece, target):
        return pltpu.make_async_remote_copy(
            src_ref=mixed.at[piece, target],
            dst_ref=(gathered.at[piece, my_col] if piece < pieces - 1 else lines.at[my_col]),
            send_sem=col_send.at[piece],
            recv_sem=col_recv.at[piece],
            device_id={col_name: target},
            device_id_type=MESH,
        )

    def col_all(piece):
        part = pl.ds(0, cols - 1)
        return pltpu.make_async_remote_copy(
            src_ref=mixed.at[piece, part],
            dst_ref=(gathered.at[piece, part] if piece < pieces - 1 else lines.at[part]),
            send_sem=col_send.at[piece],
            recv_sem=col_recv.at[piece],
            device_id={col_name: my_col},
            device_id_type=MESH,
        )

    def send_to(least, most, some):
        for piece in some:

            def step(t, carry, piece=piece):
                row_copy(piece, t).start()
                return carry

            lax.fori_loop(least, most, step, 0)

    everything = range(pieces)
    front = jnp.minimum(mine, 1) * GROUP
    near_high = (mine + 2) * GROUP
    with jax.named_scope("load"):
        pltpu.make_async_copy(hx_hbm, hx, in_sem.at[0]).wait()
        for f in range(fields):
            pltpu.make_async_copy(xin.at[f], xin.at[f], in_sem.at[1 + f]).wait()
    for f in range(fields):
        cut = [
            split(xin[f, b].reshape(share_z * share_y, LANES)) for b in range(blocks)
        ]
        mid[f] = jnp.dot(
            jnp.concatenate([part for pair in zip(*cut) for part in pair], axis=1),
            hx[...],
            preferred_element_type=F32,
        )
    for piece in everything:
        f, quad = piece // quads, piece % quads
        for block in range(rows // half):
            at = (quad * (rows // half) + block) * LANES
            tiles = [
                mid[f, z * share_y : (z + 1) * share_y, at : at + LANES] for z in range(share_z)
            ]
            keep = lane < LANES // 2
            tiles = [
                jnp.where(keep, a, b) + pltpu.roll(jnp.where(keep, b, a), LANES // 2, 1)
                for a, b in zip(tiles[:half], tiles[half:])
            ]
            unit = 1
            while unit < half:
                radix = min(4, half // unit)
                place = lane // unit % radix
                turned = list(tiles)
                for i in range(half):
                    own = i // unit % radix
                    for other in range(radix):
                        source = tiles[i + (other - own) * unit]
                        if other != own:
                            source = pltpu.roll(source, (other - own) * unit % LANES, 1)
                        turned[i] = source if other == 0 else jnp.where(place == other, source, turned[i])
                tiles = turned
                unit *= radix
            for i in range(half):
                send[piece, block * half + i] = tiles[i]
        if quad < quads - 1:
            continue
        if f == 0:
            pl.when(~soon & ~is_middle)(meet)
        with jax.named_scope(f"near{f}"):

            @pl.when(~is_middle)
            def _():
                for some in range(f * quads, (f + 1) * quads):
                    send_to(0, front, [some])

            for some in range(f * quads, (f + 1) * quads):
                recv[some, me] = send[some, me]

    @pl.when(is_middle)
    def _():
        meet()
        for piece in everything:
            send_to(near_high - GROUP, near_high, [piece])
            send_to(0, front, [piece])

    send_to(front, me, everything)
    for g in [*range(middle), *range(middle + 1, groups), middle]:
        least, most = g * GROUP, (g + 1) * GROUP
        first = jnp.maximum(least, me + 1)

        @pl.when((first < most) & ~(is_middle & (mine == g - 1)))
        def _():
            with jax.named_scope(f"ready{g}"):
                pl.semaphore_wait(row_ready.at[g], most - first)
            send_to(first, most, everything)

    for copy in fetches:
        copy.wait()
    tall_x[...] = jnp.broadcast_to(sx[...], (LANES, nx)).T
    tall_y[...] = jnp.broadcast_to(sy[...], (LANES, ny)).T
    part_y = tall_y[pl.ds(my_col * half_y, half_y), :1]
    for x in range(share_x):
        part_x = tall_x[pl.ds(me * share_x + x, 1), :1]
        at = x % width * padded(nz)
        scale[x // width, :, at : at + nz] = 1.0 / (part_x + part_y + sz[...])

    @pl.when(my_col < cols - 1)
    def _():
        pl.semaphore_wait(col_ready, cols - 1 - my_col)

    for piece in everything:
        with jax.named_scope(f"rowwait{piece}"):
            row_all(piece).wait_recv()
        high, low = split(recv[piece].reshape(ny, LANES))
        both = jnp.dot(
            hy[...], jnp.concatenate([high, low], axis=0), preferred_element_type=F32
        )
        both = both[:ny] + both[ny:]
        mixed[piece] = both.reshape(cols, half_y, LANES)
        for k in range(1, cols):
            col_copy(piece, (my_col + k) % cols).start()
        if piece < pieces - 1:
            gathered[piece, my_col] = mixed[piece, my_col]
        else:
            lines[my_col] = mixed[piece, my_col]

    for piece in everything:
        with jax.named_scope(f"colwait{piece}"):
            row_all(piece).wait_send()
            col_all(piece).wait_send()
            col_all(piece).wait_recv()
        if piece < pieces - 1:
            last_axis(gathered.at[piece], scale[piece % quads], wz, early.at[piece])


def last_axis(lines, scale, wz, out):
    cols, half_y, _ = lines.shape
    width, _, nz = out.shape
    line = jnp.concatenate([lines[c] for c in range(cols)], axis=1)
    high, low = split(line)
    both = jnp.dot(jnp.concatenate([high, low], axis=0), wz[0], preferred_element_type=F32)
    done = both[:half_y] + both[half_y:]
    done = done + jnp.dot(high, wz[1], preferred_element_type=F32)
    done = done * scale
    for j in range(width):
        out[j] = done[:, j * padded(nz) : j * padded(nz) + nz]


def last_kernel(lines, scale, early, wz, out, held, out_sem):
    pieces = early.shape[0] + 1
    quads, width = scale.shape[0], held.shape[0]
    copies = []
    for piece in range(pieces):
        if piece == pieces - 1:
            last_axis(lines, scale[piece % quads], wz, held)
        source = early.at[piece] if piece < pieces - 1 else held
        place = out.at[piece // quads, pl.ds(piece % quads * width, width)]
        copy = pltpu.make_async_copy(source, place, out_sem.at[piece])
        copy.start()
        copies.append(copy)
    with jax.named_scope("outwait"):
        for copy in copies:
            copy.wait()


def on_device(rows, cols, species, symbol_x, symbol_y, symbol_z):
    fields, nx, share_y, share_z = species.shape
    ny, nz = symbol_y.shape[0], symbol_z.shape[0]
    share_x, half_y = nx // rows, ny // cols
    width = LANES // share_z
    quads = share_x // width
    pieces = fields * quads
    hx, hy, wz = (jnp.asarray(t) for t in tables(rows, nx, ny, nz, share_z))
    dma = pltpu.SemaphoreType.DMA
    regular = pltpu.SemaphoreType.REGULAR
    width_z = width * padded(nz)
    vmem = pl.BlockSpec(memory_space=pltpu.VMEM)
    lines, scale, early = pl.pallas_call(
        functools.partial(kernel, rows, cols, ("row", "col")),
        out_shape=(
            jax.ShapeDtypeStruct((cols, half_y, LANES), F32),
            jax.ShapeDtypeStruct((quads, half_y, width_z), F32),
            jax.ShapeDtypeStruct((pieces - 1, width, half_y, nz), F32),
        ),
        in_specs=[pl.BlockSpec(memory_space=pl.ANY)] * 7,
        out_specs=(vmem, vmem, vmem),
        scratch_shapes=[
            pltpu.VMEM((fields, nx // LANES, share_z, share_y, LANES), F32),
            pltpu.VMEM((fields, share_y * share_z, 2 * nx), F32),
            pltpu.VMEM(hx.shape, BF16),
            pltpu.VMEM(hy.shape, BF16),
            pltpu.VMEM(wz.shape, BF16),
            pltpu.VMEM((1, nx), F32),
            pltpu.VMEM((1, ny), F32),
            pltpu.VMEM((1, nz), F32),
            pltpu.VMEM((pieces, rows, share_y, LANES), F32),
            pltpu.VMEM((pieces, rows, share_y, LANES), F32),
            pltpu.VMEM((pieces, cols, half_y, LANES), F32),
            pltpu.VMEM((pieces - 1, cols, half_y, LANES), F32),
            pltpu.VMEM((nx, LANES), F32),
            pltpu.VMEM((ny, LANES), F32),
            dma((fields + 6,)),
            dma((pieces,)),
            dma((pieces,)),
            dma((pieces,)),
            dma((pieces,)),
            regular((rows // GROUP,)),
            regular,
        ],
        compiler_params=pltpu.CompilerParams(collective_id=0, has_side_effects=True, vmem_limit_bytes=24 * 2**20),
    )(
        *(pltpu.with_memory_space_constraint(v, pltpu.HBM) for v in (jnp.transpose(species, (0, 2, 3, 1)), hx, hy,
        wz, symbol_x[None, :], symbol_y[None, :], symbol_z[None, :])),
    )
    return pl.pallas_call(
        last_kernel,
        out_shape=jax.ShapeDtypeStruct((fields, share_x, half_y, nz), F32),
        in_specs=[vmem, vmem, vmem, vmem],
        out_specs=pl.BlockSpec(memory_space=pl.ANY),
        scratch_shapes=[pltpu.VMEM((width, half_y, nz), F32), dma((pieces,))],
        compiler_params=pltpu.CompilerParams(vmem_limit_bytes=24 * 2**20),
    )(lines, scale, early, wz)


def solution(mesh):
    rows, cols = mesh.shape["row"], mesh.shape["col"]
    in_specs = (P(None, None, "row", "col"), P(), P(), P())
    out_specs = P(None, "row", "col", None)
    return jax.shard_map(
        functools.partial(on_device, rows, cols),
        mesh=mesh, in_specs=in_specs, out_specs=out_specs, check_vma=False,
    )
```

time: 18 us -> 16.6 us (0.922)
  Pallas kernels: 17.8 us -> 16.4 us
    pallas_call x1, Pallas kernels: 16.7 us -> 15.5 us  [on_device(): pl.pallas_call(functools.partial(kernel, rows, cols, ('row', 'col')), out...]
    pallas_call x1, Pallas kernels: 1.14 us -> 0.91 us  [on_device(): pl.pallas_call(last_kernel, out_shape=jax.ShapeDtypeStruct((fields, share...]
where the time goes in v2:
time: 16.6 us; the launch traced here: 16.4 us
  Pallas kernels  16.4 us (99%)
    pallas_call x1, Pallas kernels, on_device(): pl.pallas_call(functools.partial(kernel, rows, cols, ('row', 'col')), out...  15.5 us
    pallas_call x1, Pallas kernels, on_device(): pl.pallas_call(last_kernel, out_shape=jax.ShapeDtypeStruct((fields, share...  0.91 us

profile of v2, /device:TPU:0, one launch (start us, length us, event | category | flops | bytes accessed | tf_op | source)
XLA Modules:
  0.0 16.4 jit_solution(11469979877581045992)
XLA Ops:
  0.0 0.0 copy-start
  0.0 15.5 %shard_map.73 = (f32[2,64,128]{2,1,0:T(8,128)S(1)}, f32[2,64,512]{2,1,0:T(8,128)S(1)}, f32[3,4,64,64]{3,2,1,0:T(8,128)S(1)}) custom-call(f32[2,8,32,128]{3,2,1,0:T(8,128)} %bitcast.4, bf16[256,256]{1,0:T(8,128)(2,1)} %constant.6.clone.hx_hbm, bf16[256,256]{1,0:T(8,128)(2,1)} %constant.7.clone.hy_hbm, bf16[2,256,512]{2,1,0:T(8,128)(2,1)} %constant.8.clone.wz_hbm.wz, ...), custom_call_target="tpu_custom_call" | custom-call | tf_op jit(solution)/shard_map/pallas_call | solution.py:352
  15.5 0.0 copy-done
  15.5 0.9 %shard_map.74 = f32[2,8,64,64]{3,2,1,0:T(8,128)} custom-call(f32[2,64,128]{2,1,0:T(8,128)S(1)} %get-tuple-element.8.lines, f32[2,64,512]{2,1,0:T(8,128)S(1)} %get-tuple-element.9.scale, f32[3,4,64,64]{3,2,1,0:T(8,128)S(1)} %get-tuple-element.10.early, bf16[2,256,512]{2,1,0:T(8,128)(2,1)S(1)} %copy-done), custom_call_target="tpu_custom_call" | custom-call | tf_op jit(solution)/shard_map/pallas_call | solution.py:389
Async XLA Ops:
  0.0 15.5 %copy-start = (bf16[2,256,512]{2,1,0:T(8,128)(2,1)S(1)}, bf16[2,256,512]{2,1,0:T(8,128)(2,1)}, u32[]{:S(2)}) copy-start(bf16[2,256,512]{2,1,0:T(8,128)(2,1)} %constant.8.clone.wz_hbm.wz) | copy-start | bytes 1572868

commit v3 on v2

--- a/solution.py
+++ b/solution.py
@@ -64,7 +64,7 @@
     species, hx_hbm, hy_hbm, wz_hbm, sx_hbm, sy_hbm, sz_hbm,
     lines, scale, early,
     xin, mid, hx, hy, wz, sx, sy, sz, send, recv, mixed, gathered, tall_x, tall_y,
-    in_sem, row_send, row_recv, col_send, col_recv, row_ready, col_ready,
+    in_sem, row_send, row_recv, col_send, col_recv, row_ready,
 ):
     row_name, col_name = names
     fields, _, _, nx = species.shape
@@ -74,7 +74,7 @@
     width, half = LANES // share_z, share_z // 2
     quads = share_x // width
     pieces = fields * quads
-    groups = row_ready.shape[0]
+    groups = rows // GROUP
     middle = groups // 2 - 1
     me, my_col = lax.axis_index(row_name), lax.axis_index(col_name)
     mine = me // GROUP
@@ -91,7 +91,7 @@
         for b in range(blocks):
             for y in range(share_y):
                 pltpu.make_async_copy(
-                    species.at[f, y, :, pl.ds(b * LANES, LANES)], xin.at[f, b, :, y, :], in_sem.at[1 + f]
+                    species.at[f, y, :, pl.ds(b * LANES, LANES)], xin.at[f, b, :, y, :], in_sem.at[f]
                 ).start()
 
     barrier = pltpu.get_barrier_semaphore()
@@ -104,29 +104,30 @@
         pl.semaphore_signal(barrier, inc=1, device_id={col_name: t}, device_id_type=MESH)
         return carry
 
-    is_middle = mine == middle
-    past = mine == middle + 1
+    low = mine <= middle
     back = (mine - 1) * GROUP
+    past = (mine > 0) & (mine <= middle + 1)
     lax.fori_loop(jnp.where(past, back, 0), jnp.where(past, back + GROUP, 0), greet_row, 0)
     lax.fori_loop(me + 1, rows, greet_row, 0)
     lax.fori_loop(my_col + 1, cols, greet_col, 0)
     rest = ((hy_hbm, hy), (wz_hbm, wz), (sx_hbm, sx), (sy_hbm, sy), (sz_hbm, sz))
     fetches = [
-        pltpu.make_async_copy(a, b, in_sem.at[1 + fields + i]) for i, (a, b) in enumerate(rest)
+        pltpu.make_async_copy(a, b, in_sem.at[fields]) for a, b in rest
     ]
     for copy in fetches:
         copy.start()
 
     def ready_row(t, carry):
-        pl.semaphore_signal(row_ready.at[mine], inc=1, device_id={row_name: t}, device_id_type=MESH)
+        other = (~low & (t < (middle + 1) * GROUP)).astype(jnp.int32)
+        pl.semaphore_signal(row_ready.at[other], inc=1, device_id={row_name: t}, device_id_type=MESH)
         return carry
 
     def ready_col(t, carry):
-        pl.semaphore_signal(col_ready, inc=1, device_id={col_name: t}, device_id_type=MESH)
+        pl.semaphore_signal(row_ready.at[0], inc=1, device_id={col_name: t}, device_id_type=MESH)
         return carry
 
     def meet():
-        count = me + my_col + jnp.where(is_middle, GROUP, 0)
+        count = me + my_col + jnp.where(low, GROUP, 0)
 
         @pl.when(count > 0)
         def _():
@@ -137,7 +138,7 @@
         lax.fori_loop(jnp.where(past, mine * GROUP, me), me, ready_row, 0)
         lax.fori_loop(0, my_col, ready_col, 0)
 
-    soon = (me % GROUP >= GROUP // 2) & ~is_middle
+    soon = (me % GROUP >= GROUP // 2) & ~low
     pl.when(soon)(meet)
 
     lane = lax.broadcasted_iota(jnp.int32, (share_y, LANES), 1)
@@ -146,7 +147,7 @@
         return pltpu.make_async_remote_copy(
             src_ref=send.at[piece, target],
             dst_ref=recv.at[piece, me],
-            send_sem=row_send.at[piece],
+            send_sem=row_send,
             recv_sem=row_recv.at[piece],
             device_id={row_name: target},
             device_id_type=MESH,
@@ -156,7 +157,7 @@
         return pltpu.make_async_remote_copy(
             src_ref=send.at[piece, pl.ds(0, rows - 1)],
             dst_ref=recv.at[piece, pl.ds(0, rows - 1)],
-            send_sem=row_send.at[piece],
+            send_sem=row_send,
             recv_sem=row_recv.at[piece],
             device_id={row_name: me},
             device_id_type=MESH,
@@ -166,7 +167,7 @@
         return pltpu.make_async_remote_copy(
             src_ref=mixed.at[piece, target],
             dst_ref=(gathered.at[piece, my_col] if piece < pieces - 1 else lines.at[my_col]),
-            send_sem=col_send.at[piece],
+            send_sem=col_send,
             recv_sem=col_recv.at[piece],
             device_id={col_name: target},
             device_id_type=MESH,
@@ -177,7 +178,7 @@
         return pltpu.make_async_remote_copy(
             src_ref=mixed.at[piece, part],
             dst_ref=(gathered.at[piece, part] if piece < pieces - 1 else lines.at[part]),
-            send_sem=col_send.at[piece],
+            send_sem=col_send,
             recv_sem=col_recv.at[piece],
             device_id={col_name: my_col},
             device_id_type=MESH,
@@ -195,19 +196,23 @@
     everything = range(pieces)
     front = jnp.minimum(mine, 1) * GROUP
     near_high = (mine + 2) * GROUP
+    def product(f):
+        cut = [
+            split(xin[f, b].reshape(share_z * share_y, LANES)) for b in range(blocks)
+        ]
+        line = jnp.concatenate([part for pair in zip(*cut) for part in pair], axis=1)
+        size = half * share_y
+        for at in (0, size):
+            mid[f, at : at + size] = jnp.dot(
+                line[at : at + size], hx[...], preferred_element_type=F32
+            )
+
     with jax.named_scope("load"):
         pltpu.make_async_copy(hx_hbm, hx, in_sem.at[0]).wait()
         for f in range(fields):
-            pltpu.make_async_copy(xin.at[f], xin.at[f], in_sem.at[1 + f]).wait()
+            pltpu.make_async_copy(xin.at[f], xin.at[f], in_sem.at[f]).wait()
     for f in range(fields):
-        cut = [
-            split(xin[f, b].reshape(share_z * share_y, LANES)) for b in range(blocks)
-        ]
-        mid[f] = jnp.dot(
-            jnp.concatenate([part for pair in zip(*cut) for part in pair], axis=1),
-            hx[...],
-            preferred_element_type=F32,
-        )
+        product(f)
     for piece in everything:
         f, quad = piece // quads, piece % quads
         for block in range(rows // half):
@@ -239,10 +244,10 @@
         if quad < quads - 1:
             continue
         if f == 0:
-            pl.when(~soon & ~is_middle)(meet)
+            pl.when(~soon & ~low)(meet)
         with jax.named_scope(f"near{f}"):
 
-            @pl.when(~is_middle)
+            @pl.when(~low)
             def _():
                 for some in range(f * quads, (f + 1) * quads):
                     send_to(0, front, [some])
@@ -250,23 +255,43 @@
             for some in range(f * quads, (f + 1) * quads):
                 recv[some, me] = send[some, me]
 
-    @pl.when(is_middle)
+    @pl.when(low)
     def _():
         meet()
         for piece in everything:
+            send_to(0, front, [piece])
             send_to(near_high - GROUP, near_high, [piece])
-            send_to(0, front, [piece])
-
-    send_to(front, me, everything)
-    for g in [*range(middle), *range(middle + 1, groups), middle]:
-        least, most = g * GROUP, (g + 1) * GROUP
-        first = jnp.maximum(least, me + 1)
-
-        @pl.when((first < most) & ~(is_middle & (mine == g - 1)))
+
+    across = (jnp.where(mine > 0, GROUP, 0), jnp.minimum(mine, middle + 1) * GROUP)
+    pl.when(mine <= middle + 1)(lambda: send_to(*across, everything))
+    for g in reversed(range(middle + 1, groups)):
+
+        @pl.when(g < mine)
         def _():
-            with jax.named_scope(f"ready{g}"):
-                pl.semaphore_wait(row_ready.at[g], most - first)
-            send_to(first, most, everything)
+            send_to(g * GROUP, (g + 1) * GROUP, everything)
+
+    pl.when(mine > middle + 1)(lambda: send_to(*across, everything))
+    send_to(mine * GROUP, me, everything)
+
+    half_end = jnp.where(low, (middle + 1) * GROUP, rows)
+    last = jnp.minimum((mine + 1) * GROUP, half_end)
+    greeted = jnp.where(low, jnp.minimum((mine + 2) * GROUP, half_end), last)
+    count = half_end - me - 1 - (greeted - last) + cols - 1 - my_col
+
+    @pl.when(count > 0)
+    def _():
+        with jax.named_scope("ready0"):
+            pl.semaphore_wait(row_ready.at[0], count)
+
+    send_to(me + 1, last, everything)
+    send_to(greeted, half_end, everything)
+
+    @pl.when(low)
+    def _():
+        far = jnp.maximum(mine + 2, middle + 1) * GROUP
+        with jax.named_scope("ready1"):
+            pl.semaphore_wait(row_ready.at[1], rows - far)
+        send_to(far, rows, everything)
 
     for copy in fetches:
         copy.wait()
@@ -278,33 +303,36 @@
         at = x % width * padded(nz)
         scale[x // width, :, at : at + nz] = 1.0 / (part_x + part_y + sz[...])
 
-    @pl.when(my_col < cols - 1)
-    def _():
-        pl.semaphore_wait(col_ready, cols - 1 - my_col)
-
     for piece in everything:
         with jax.named_scope(f"rowwait{piece}"):
             row_all(piece).wait_recv()
         high, low = split(recv[piece].reshape(ny, LANES))
-        both = jnp.dot(
-            hy[...], jnp.concatenate([high, low], axis=0), preferred_element_type=F32
-        )
-        both = both[:ny] + both[ny:]
-        mixed[piece] = both.reshape(cols, half_y, LANES)
+        stacked = jnp.concatenate([high, low], axis=0)
+        parts = []
+        for k in range(1, cols + 1):
+            at = pl.multiple_of((my_col + k) % cols * half_y, half_y)
+            table = jnp.concatenate([hy[pl.ds(at, half_y), :], hy[pl.ds(ny + at, half_y), :]], axis=0)
+            both = jnp.dot(table, stacked, preferred_element_type=F32)
+            parts.append(both[:half_y] + both[half_y:])
+        for k in range(1, cols):
+            mixed[piece, (my_col + k) % cols] = parts[k - 1]
         for k in range(1, cols):
             col_copy(piece, (my_col + k) % cols).start()
         if piece < pieces - 1:
-            gathered[piece, my_col] = mixed[piece, my_col]
+            gathered[piece, my_col] = parts[-1]
         else:
-            lines[my_col] = mixed[piece, my_col]
+            lines[my_col] = parts[-1]
 
     for piece in everything:
         with jax.named_scope(f"colwait{piece}"):
-            row_all(piece).wait_send()
-            col_all(piece).wait_send()
             col_all(piece).wait_recv()
         if piece < pieces - 1:
             last_axis(gathered.at[piece], scale[piece % quads], wz, early.at[piece])
+        if piece == pieces - 2:
+            sent = send.at[:, pl.ds(0, rows - 1)]
+            pltpu.make_async_copy(sent, sent, row_send).wait()
+    sent = mixed.at[:, pl.ds(0, cols - 1)]
+    pltpu.make_async_copy(sent, sent, col_send).wait()
 
 
 def last_axis(lines, scale, wz, out):
@@ -373,13 +401,12 @@
             pltpu.VMEM((pieces - 1, cols, half_y, LANES), F32),
             pltpu.VMEM((nx, LANES), F32),
             pltpu.VMEM((ny, LANES), F32),
-            dma((fields + 6,)),
+            dma((fields + 1,)),
+            dma,
             dma((pieces,)),
+            dma,
             dma((pieces,)),
-            dma((pieces,)),
-            dma((pieces,)),
-            regular((rows // GROUP,)),
-            regular,
+            regular((2,)),
         ],
         compiler_params=pltpu.CompilerParams(collective_id=0, has_side_effects=True, vmem_limit_bytes=24 * 2**20),
     )(

time: 16.6 us -> 16.1 us (0.970)
  Pallas kernels: 16.4 us -> 15.8 us
    pallas_call x1, Pallas kernels: 15.5 us -> 14.9 us  [on_device(): pl.pallas_call(functools.partial(kernel, rows, cols, ('row', 'col')), out...]
where the time goes in v3:
time: 16.1 us; the launch traced here: 15.8 us
  Pallas kernels  15.8 us (98%)
    pallas_call x1, Pallas kernels, on_device(): pl.pallas_call(functools.partial(kernel, rows, cols, ('row', 'col')), out...  14.9 us
    pallas_call x1, Pallas kernels, on_device(): pl.pallas_call(last_kernel, out_shape=jax.ShapeDtypeStruct((fields, share...  0.91 us

profile of v3, /device:TPU:0, one launch (start us, length us, event | category | flops | bytes accessed | tf_op | source)
XLA Modules:
  0.0 15.8 jit_solution(350610912011468941)
XLA Ops:
  0.0 0.0 copy-start
  0.0 14.9 %shard_map.73 = (f32[2,64,128]{2,1,0:T(8,128)S(1)}, f32[2,64,512]{2,1,0:T(8,128)S(1)}, f32[3,4,64,64]{3,2,1,0:T(8,128)S(1)}) custom-call(f32[2,8,32,128]{3,2,1,0:T(8,128)} %bitcast.4, bf16[256,256]{1,0:T(8,128)(2,1)} %constant.6.clone.hx_hbm, bf16[256,256]{1,0:T(8,128)(2,1)} %constant.7.clone.hy_hbm, bf16[2,256,512]{2,1,0:T(8,128)(2,1)} %constant.8.clone.wz_hbm.wz, ...), custom_call_target="tpu_custom_call" | custom-call | tf_op jit(solution)/shard_map/pallas_call | solution.py:380
  14.9 0.0 copy-done
  14.9 0.9 %shard_map.74 = f32[2,8,64,64]{3,2,1,0:T(8,128)} custom-call(f32[2,64,128]{2,1,0:T(8,128)S(1)} %get-tuple-element.8.lines, f32[2,64,512]{2,1,0:T(8,128)S(1)} %get-tuple-element.9.scale, f32[3,4,64,64]{3,2,1,0:T(8,128)S(1)} %get-tuple-element.10.early, bf16[2,256,512]{2,1,0:T(8,128)(2,1)S(1)} %copy-done), custom_call_target="tpu_custom_call" | custom-call | tf_op jit(solution)/shard_map/pallas_call | solution.py:416
Async XLA Ops:
  0.0 14.9 %copy-start = (bf16[2,256,512]{2,1,0:T(8,128)(2,1)S(1)}, bf16[2,256,512]{2,1,0:T(8,128)(2,1)}, u32[]{:S(2)}) copy-start(bf16[2,256,512]{2,1,0:T(8,128)(2,1)} %constant.8.clone.wz_hbm.wz) | copy-start | bytes 1572868

commit v4 on v3

--- a/solution.py
+++ b/solution.py
@@ -86,14 +86,16 @@
             pltpu.make_async_copy(source.at[span], target.at[span], semaphore).start()
 
     blocks = nx // LANES
-    fetch(hx_hbm, hx, in_sem.at[0], 4)
-    for f in range(fields):
+    def fetch_field(f):
         for b in range(blocks):
             for y in range(share_y):
                 pltpu.make_async_copy(
                     species.at[f, y, :, pl.ds(b * LANES, LANES)], xin.at[f, b, :, y, :], in_sem.at[f]
                 ).start()
 
+    fetch(hx_hbm, hx, in_sem.at[0], 4)
+    fetch_field(0)
+
     barrier = pltpu.get_barrier_semaphore()
 
     def greet_row(t, carry):
@@ -107,9 +109,13 @@
     low = mine <= middle
     back = (mine - 1) * GROUP
     past = (mine > 0) & (mine <= middle + 1)
-    lax.fori_loop(jnp.where(past, back, 0), jnp.where(past, back + GROUP, 0), greet_row, 0)
+    first_half = me % GROUP < GROUP // 2
+    back_from = back + jnp.where(first_half, 0, GROUP // 2)
+    lax.fori_loop(jnp.where(past, back_from, 0), jnp.where(past, back + GROUP, 0), greet_row, 0)
     lax.fori_loop(me + 1, rows, greet_row, 0)
     lax.fori_loop(my_col + 1, cols, greet_col, 0)
+    for f in range(1, fields):
+        fetch_field(f)
     rest = ((hy_hbm, hy), (wz_hbm, wz), (sx_hbm, sx), (sy_hbm, sy), (sz_hbm, sz))
     fetches = [
         pltpu.make_async_copy(a, b, in_sem.at[fields]) for a, b in rest
@@ -119,6 +125,7 @@
 
     def ready_row(t, carry):
         other = (~low & (t < (middle + 1) * GROUP)).astype(jnp.int32)
+        other = jnp.where(past & (t >= back), jnp.where(t < back + GROUP, 2, other), other)
         pl.semaphore_signal(row_ready.at[other], inc=1, device_id={row_name: t}, device_id_type=MESH)
         return carry
 
@@ -127,14 +134,14 @@
         return carry
 
     def meet():
-        count = me + my_col + jnp.where(low, GROUP, 0)
+        count = me + my_col + jnp.where(low, jnp.where(first_half, GROUP // 2, GROUP), 0)
 
         @pl.when(count > 0)
         def _():
             with jax.named_scope("barrier"):
                 pl.semaphore_wait(barrier, count)
 
-        lax.fori_loop(0, jnp.where(past, back, me), ready_row, 0)
+        lax.fori_loop(0, jnp.where(past, back_from, me), ready_row, 0)
         lax.fori_loop(jnp.where(past, mine * GROUP, me), me, ready_row, 0)
         lax.fori_loop(0, my_col, ready_col, 0)
 
@@ -207,14 +214,18 @@
                 line[at : at + size], hx[...], preferred_element_type=F32
             )
 
+    def load(f):
+        pltpu.make_async_copy(xin.at[f], xin.at[f], in_sem.at[f]).wait()
+
     with jax.named_scope("load"):
         pltpu.make_async_copy(hx_hbm, hx, in_sem.at[0]).wait()
-        for f in range(fields):
-            pltpu.make_async_copy(xin.at[f], xin.at[f], in_sem.at[f]).wait()
-    for f in range(fields):
-        product(f)
+        load(0)
+    product(0)
     for piece in everything:
         f, quad = piece // quads, piece % quads
+        if quad == quads - 1 and f + 1 < fields:
+            load(f + 1)
+            product(f + 1)
         for block in range(rows // half):
             at = (quad * (rows // half) + block) * LANES
             tiles = [
@@ -241,37 +252,44 @@
                 unit *= radix
             for i in range(half):
                 send[piece, block * half + i] = tiles[i]
-        if quad < quads - 1:
-            continue
-        if f == 0:
+        if piece == 0:
             pl.when(~soon & ~low)(meet)
-        with jax.named_scope(f"near{f}"):
+        with jax.named_scope(f"near{piece}"):
 
             @pl.when(~low)
             def _():
-                for some in range(f * quads, (f + 1) * quads):
-                    send_to(0, front, [some])
-
-            for some in range(f * quads, (f + 1) * quads):
-                recv[some, me] = send[some, me]
-
-    @pl.when(low)
+                send_to(0, front, [piece])
+
+            if piece >= quads - 1:
+                some = range(quads) if piece == quads - 1 else [piece]
+
+                @pl.when(low)
+                def _():
+                    if piece == quads - 1:
+                        meet()
+                    for one in some:
+                        send_to(0, front, [one])
+                        send_to(near_high - GROUP, near_high - jnp.where(first_half, GROUP // 2, 0), [one])
+
+            recv[piece, me] = send[piece, me]
+
+    across = (jnp.where(mine > 0, GROUP, 0), jnp.minimum(mine, middle + 1) * GROUP)
+    for f in range(fields):
+        some = range(f * quads, (f + 1) * quads)
+        for g in reversed(range(middle + 1, groups)):
+
+            @pl.when(g < mine)
+            def _():
+                send_to(g * GROUP, (g + 1) * GROUP, some)
+
+        send_to(*across, some)
+    send_to(mine * GROUP, me, everything)
+
+    @pl.when(low & first_half)
     def _():
-        meet()
-        for piece in everything:
-            send_to(0, front, [piece])
-            send_to(near_high - GROUP, near_high, [piece])
-
-    across = (jnp.where(mine > 0, GROUP, 0), jnp.minimum(mine, middle + 1) * GROUP)
-    pl.when(mine <= middle + 1)(lambda: send_to(*across, everything))
-    for g in reversed(range(middle + 1, groups)):
-
-        @pl.when(g < mine)
-        def _():
-            send_to(g * GROUP, (g + 1) * GROUP, everything)
-
-    pl.when(mine > middle + 1)(lambda: send_to(*across, everything))
-    send_to(mine * GROUP, me, everything)
+        with jax.named_scope("ready2"):
+            pl.semaphore_wait(row_ready.at[2], GROUP // 2)
+        send_to(near_high - GROUP // 2, near_high, everything)
 
     half_end = jnp.where(low, (middle + 1) * GROUP, rows)
     last = jnp.minimum((mine + 1) * GROUP, half_end)
@@ -406,7 +424,7 @@
             dma((pieces,)),
             dma,
             dma((pieces,)),
-            regular((2,)),
+            regular((3,)),
         ],
         compiler_params=pltpu.CompilerParams(collective_id=0, has_side_effects=True, vmem_limit_bytes=24 * 2**20),
     )(

time: 16.1 us -> 15.9 us (0.988)
  no operation moved by 1% of the time
where the time goes in v4:
time: 15.9 us; the launch traced here: 15.7 us
  Pallas kernels  15.7 us (99%)
    pallas_call x1, Pallas kernels, on_device(): pl.pallas_call(functools.partial(kernel, rows, cols, ('row', 'col')), out...  14.8 us
    pallas_call x1, Pallas kernels, on_device(): pl.pallas_call(last_kernel, out_shape=jax.ShapeDtypeStruct((fields, share...  0.91 us

profile of v4, /device:TPU:0, one launch (start us, length us, event | category | flops | bytes accessed | tf_op | source)
XLA Modules:
  0.0 15.7 jit_solution(18206382042780257536)
XLA Ops:
  0.0 0.0 copy-start
  0.0 14.8 %shard_map.73 = (f32[2,64,128]{2,1,0:T(8,128)S(1)}, f32[2,64,512]{2,1,0:T(8,128)S(1)}, f32[3,4,64,64]{3,2,1,0:T(8,128)S(1)}) custom-call(f32[2,8,32,128]{3,2,1,0:T(8,128)} %bitcast.4, bf16[256,256]{1,0:T(8,128)(2,1)} %constant.6.clone.hx_hbm, bf16[256,256]{1,0:T(8,128)(2,1)} %constant.7.clone.hy_hbm, bf16[2,256,512]{2,1,0:T(8,128)(2,1)} %constant.8.clone.wz_hbm.wz, ...), custom_call_target="tpu_custom_call" | custom-call | tf_op jit(solution)/shard_map/pallas_call | solution.py:398
  14.8 0.0 copy-done
  14.8 0.9 %shard_map.74 = f32[2,8,64,64]{3,2,1,0:T(8,128)} custom-call(f32[2,64,128]{2,1,0:T(8,128)S(1)} %get-tuple-element.8.lines, f32[2,64,512]{2,1,0:T(8,128)S(1)} %get-tuple-element.9.scale, f32[3,4,64,64]{3,2,1,0:T(8,128)S(1)} %get-tuple-element.10.early, bf16[2,256,512]{2,1,0:T(8,128)(2,1)S(1)} %copy-done), custom_call_target="tpu_custom_call" | custom-call | tf_op jit(solution)/shard_map/pallas_call | solution.py:434
Async XLA Ops:
  0.0 14.8 %copy-start = (bf16[2,256,512]{2,1,0:T(8,128)(2,1)S(1)}, bf16[2,256,512]{2,1,0:T(8,128)(2,1)}, u32[]{:S(2)}) copy-start(bf16[2,256,512]{2,1,0:T(8,128)(2,1)} %constant.8.clone.wz_hbm.wz) | copy-start | bytes 1572868

commit v5 on v4

--- a/solution.py
+++ b/solution.py
@@ -201,7 +201,7 @@
             lax.fori_loop(least, most, step, 0)
 
     everything = range(pieces)
-    front = jnp.minimum(mine, 1) * GROUP
+    front = jnp.minimum(mine, 1) * (GROUP // 2)
     near_high = (mine + 2) * GROUP
     def product(f):
         cut = [
@@ -274,14 +274,18 @@
             recv[piece, me] = send[piece, me]
 
     across = (jnp.where(mine > 0, GROUP, 0), jnp.minimum(mine, middle + 1) * GROUP)
-    for f in range(fields):
-        some = range(f * quads, (f + 1) * quads)
+
+    def send_near(some):
         for g in reversed(range(middle + 1, groups)):
 
             @pl.when(g < mine)
             def _():
                 send_to(g * GROUP, (g + 1) * GROUP, some)
 
+    for f in range(fields):
+        some = range(f * quads, (f + 1) * quads)
+        send_to(front, 2 * front, some)
+        send_near(some)
         send_to(*across, some)
     send_to(mine * GROUP, me, everything)
 

time: 15.9 us -> 15.8 us (level)
  Pallas kernels: 15.7 us -> 15.5 us
    pallas_call x1, Pallas kernels: 14.8 us -> 14.6 us  [on_device(): pl.pallas_call(functools.partial(kernel, rows, cols, ('row', 'col')), out...]
where the time goes in v5:
time: 15.8 us; the launch traced here: 15.5 us
  Pallas kernels  15.5 us (98%)
    pallas_call x1, Pallas kernels, on_device(): pl.pallas_call(functools.partial(kernel, rows, cols, ('row', 'col')), out...  14.6 us
    pallas_call x1, Pallas kernels, on_device(): pl.pallas_call(last_kernel, out_shape=jax.ShapeDtypeStruct((fields, share...  0.91 us

profile of v5, /device:TPU:0, one launch (start us, length us, event | category | flops | bytes accessed | tf_op | source)
XLA Modules:
  0.0 15.5 jit_solution(2104372076119519174)
XLA Ops:
  0.0 0.0 copy-start
  0.0 14.6 %shard_map.73 = (f32[2,64,128]{2,1,0:T(8,128)S(1)}, f32[2,64,512]{2,1,0:T(8,128)S(1)}, f32[3,4,64,64]{3,2,1,0:T(8,128)S(1)}) custom-call(f32[2,8,32,128]{3,2,1,0:T(8,128)} %bitcast.4, bf16[256,256]{1,0:T(8,128)(2,1)} %constant.6.clone.hx_hbm, bf16[256,256]{1,0:T(8,128)(2,1)} %constant.7.clone.hy_hbm, bf16[2,256,512]{2,1,0:T(8,128)(2,1)} %constant.8.clone.wz_hbm.wz, ...), custom_call_target="tpu_custom_call" | custom-call | tf_op jit(solution)/shard_map/pallas_call | solution.py:402
  14.6 0.0 copy-done
  14.6 0.9 %shard_map.74 = f32[2,8,64,64]{3,2,1,0:T(8,128)} custom-call(f32[2,64,128]{2,1,0:T(8,128)S(1)} %get-tuple-element.8.lines, f32[2,64,512]{2,1,0:T(8,128)S(1)} %get-tuple-element.9.scale, f32[3,4,64,64]{3,2,1,0:T(8,128)S(1)} %get-tuple-element.10.early, bf16[2,256,512]{2,1,0:T(8,128)(2,1)S(1)} %copy-done), custom_call_target="tpu_custom_call" | custom-call | tf_op jit(solution)/shard_map/pallas_call | solution.py:438
Async XLA Ops:
  0.0 14.6 %copy-start = (bf16[2,256,512]{2,1,0:T(8,128)(2,1)S(1)}, bf16[2,256,512]{2,1,0:T(8,128)(2,1)}, u32[]{:S(2)}) copy-start(bf16[2,256,512]{2,1,0:T(8,128)(2,1)} %constant.8.clone.wz_hbm.wz) | copy-start | bytes 1572868

commit v6 on v5

--- a/solution.py
+++ b/solution.py
@@ -64,7 +64,7 @@
     species, hx_hbm, hy_hbm, wz_hbm, sx_hbm, sy_hbm, sz_hbm,
     lines, scale, early,
     xin, mid, hx, hy, wz, sx, sy, sz, send, recv, mixed, gathered, tall_x, tall_y,
-    in_sem, row_send, row_recv, col_send, col_recv, row_ready,
+    row_send, row_recv, col_send, col_recv, row_ready,
 ):
     row_name, col_name = names
     fields, _, _, nx = species.shape
@@ -86,14 +86,16 @@
             pltpu.make_async_copy(source.at[span], target.at[span], semaphore).start()
 
     blocks = nx // LANES
+    landed = (row_send, *([col_send] * (fields - 1)))
+
     def fetch_field(f):
         for b in range(blocks):
             for y in range(share_y):
                 pltpu.make_async_copy(
-                    species.at[f, y, :, pl.ds(b * LANES, LANES)], xin.at[f, b, :, y, :], in_sem.at[f]
+                    species.at[f, y, :, pl.ds(b * LANES, LANES)], xin.at[f, b, :, y, :], landed[f]
                 ).start()
 
-    fetch(hx_hbm, hx, in_sem.at[0], 4)
+    fetch(hx_hbm, hx, row_send, 4)
     fetch_field(0)
 
     barrier = pltpu.get_barrier_semaphore()
@@ -117,11 +119,7 @@
     for f in range(1, fields):
         fetch_field(f)
     rest = ((hy_hbm, hy), (wz_hbm, wz), (sx_hbm, sx), (sy_hbm, sy), (sz_hbm, sz))
-    fetches = [
-        pltpu.make_async_copy(a, b, in_sem.at[fields]) for a, b in rest
-    ]
-    for copy in fetches:
-        copy.start()
+    fetches = [pltpu.make_async_copy(a, b, col_send) for a, b in rest]
 
     def ready_row(t, carry):
         other = (~low & (t < (middle + 1) * GROUP)).astype(jnp.int32)
@@ -215,10 +213,10 @@
             )
 
     def load(f):
-        pltpu.make_async_copy(xin.at[f], xin.at[f], in_sem.at[f]).wait()
+        pltpu.make_async_copy(xin.at[f], xin.at[f], landed[f]).wait()
 
     with jax.named_scope("load"):
-        pltpu.make_async_copy(hx_hbm, hx, in_sem.at[0]).wait()
+        pltpu.make_async_copy(hx_hbm, hx, row_send).wait()
         load(0)
     product(0)
     for piece in everything:
@@ -226,6 +224,9 @@
         if quad == quads - 1 and f + 1 < fields:
             load(f + 1)
             product(f + 1)
+            if f + 2 == fields:
+                for copy in fetches:
+                    copy.start()
         for block in range(rows // half):
             at = (quad * (rows // half) + block) * LANES
             tiles = [
@@ -423,7 +424,6 @@
             pltpu.VMEM((pieces - 1, cols, half_y, LANES), F32),
             pltpu.VMEM((nx, LANES), F32),
             pltpu.VMEM((ny, LANES), F32),
-            dma((fields + 1,)),
             dma,
             dma((pieces,)),
             dma,

time: 15.8 us -> 15.7 us (level)
  no operation moved by 1% of the time
where the time goes in v6:
time: 15.7 us; the launch traced here: 15.5 us
  Pallas kernels  15.4 us (98%)
    pallas_call x1, Pallas kernels, on_device(): pl.pallas_call(functools.partial(kernel, rows, cols, ('row', 'col')), out...  14.5 us
    pallas_call x1, Pallas kernels, on_device(): pl.pallas_call(last_kernel, out_shape=jax.ShapeDtypeStruct((fields, share...  0.91 us

profile of v6, /device:TPU:0, one launch (start us, length us, event | category | flops | bytes accessed | tf_op | source)
XLA Modules:
  0.0 15.5 jit_solution(10223739805665207211)
XLA Ops:
  0.0 0.0 copy-start
  0.0 14.5 %shard_map.73 = (f32[2,64,128]{2,1,0:T(8,128)S(1)}, f32[2,64,512]{2,1,0:T(8,128)S(1)}, f32[3,4,64,64]{3,2,1,0:T(8,128)S(1)}) custom-call(f32[2,8,32,128]{3,2,1,0:T(8,128)} %bitcast.4, bf16[256,256]{1,0:T(8,128)(2,1)} %constant.6.clone.hx_hbm, bf16[256,256]{1,0:T(8,128)(2,1)} %constant.7.clone.hy_hbm, bf16[2,256,512]{2,1,0:T(8,128)(2,1)} %constant.8.clone.wz_hbm.wz, ...), custom_call_target="tpu_custom_call" | custom-call | tf_op jit(solution)/shard_map/pallas_call | solution.py:403
  14.5 0.0 copy-done
  14.6 0.9 %shard_map.74 = f32[2,8,64,64]{3,2,1,0:T(8,128)} custom-call(f32[2,64,128]{2,1,0:T(8,128)S(1)} %get-tuple-element.8.lines, f32[2,64,512]{2,1,0:T(8,128)S(1)} %get-tuple-element.9.scale, f32[3,4,64,64]{3,2,1,0:T(8,128)S(1)} %get-tuple-element.10.early, bf16[2,256,512]{2,1,0:T(8,128)(2,1)S(1)} %copy-done), custom_call_target="tpu_custom_call" | custom-call | tf_op jit(solution)/shard_map/pallas_call | solution.py:438
Async XLA Ops:
  0.0 14.5 %copy-start = (bf16[2,256,512]{2,1,0:T(8,128)(2,1)S(1)}, bf16[2,256,512]{2,1,0:T(8,128)(2,1)}, u32[]{:S(2)}) copy-start(bf16[2,256,512]{2,1,0:T(8,128)(2,1)} %constant.8.clone.wz_hbm.wz) | copy-start | bytes 1572868

commit v7 on v6

--- a/solution.py
+++ b/solution.py
@@ -283,11 +283,18 @@
             def _():
                 send_to(g * GROUP, (g + 1) * GROUP, some)
 
+    across_mid = (across[0] + across[1]) // 2
     for f in range(fields):
         some = range(f * quads, (f + 1) * quads)
         send_to(front, 2 * front, some)
-        send_near(some)
-        send_to(*across, some)
+        if f > 0:
+            send_near(some[: quads // 2])
+            send_to(across[0], across_mid, some)
+            send_near(some[quads // 2 :])
+            send_to(across_mid, across[1], some)
+        else:
+            send_near(some)
+            send_to(*across, some)
     send_to(mine * GROUP, me, everything)
 
     @pl.when(low & first_half)

time: 15.7 us -> 15.7 us (level)
  no operation moved by 1% of the time
where the time goes in v7:
time: 15.7 us; the launch traced here: 15.5 us
  Pallas kernels  15.4 us (98%)
    pallas_call x1, Pallas kernels, on_device(): pl.pallas_call(functools.partial(kernel, rows, cols, ('row', 'col')), out...  14.5 us
    pallas_call x1, Pallas kernels, on_device(): pl.pallas_call(last_kernel, out_shape=jax.ShapeDtypeStruct((fields, share...  0.91 us

profile of v7, /device:TPU:0, one launch (start us, length us, event | category | flops | bytes accessed | tf_op | source)
XLA Modules:
  0.0 15.5 jit_solution(14186531532584240498)
XLA Ops:
  0.0 0.0 copy-start
  0.0 14.5 %shard_map.73 = (f32[2,64,128]{2,1,0:T(8,128)S(1)}, f32[2,64,512]{2,1,0:T(8,128)S(1)}, f32[3,4,64,64]{3,2,1,0:T(8,128)S(1)}) custom-call(f32[2,8,32,128]{3,2,1,0:T(8,128)} %bitcast.4, bf16[256,256]{1,0:T(8,128)(2,1)} %constant.6.clone.hx_hbm, bf16[256,256]{1,0:T(8,128)(2,1)} %constant.7.clone.hy_hbm, bf16[2,256,512]{2,1,0:T(8,128)(2,1)} %constant.8.clone.wz_hbm.wz, ...), custom_call_target="tpu_custom_call" | custom-call | tf_op jit(solution)/shard_map/pallas_call | solution.py:410
  14.5 0.0 copy-done
  14.6 0.9 %shard_map.74 = f32[2,8,64,64]{3,2,1,0:T(8,128)} custom-call(f32[2,64,128]{2,1,0:T(8,128)S(1)} %get-tuple-element.8.lines, f32[2,64,512]{2,1,0:T(8,128)S(1)} %get-tuple-element.9.scale, f32[3,4,64,64]{3,2,1,0:T(8,128)S(1)} %get-tuple-element.10.early, bf16[2,256,512]{2,1,0:T(8,128)(2,1)S(1)} %copy-done), custom_call_target="tpu_custom_call" | custom-call | tf_op jit(solution)/shard_map/pallas_call | solution.py:445
Async XLA Ops:
  0.0 14.5 %copy-start = (bf16[2,256,512]{2,1,0:T(8,128)(2,1)S(1)}, bf16[2,256,512]{2,1,0:T(8,128)(2,1)}, u32[]{:S(2)}) copy-start(bf16[2,256,512]{2,1,0:T(8,128)(2,1)} %constant.8.clone.wz_hbm.wz) | copy-start | bytes 1572868

commit v8 on v7

--- a/solution.py
+++ b/solution.py
@@ -272,7 +272,6 @@
                         send_to(0, front, [one])
                         send_to(near_high - GROUP, near_high - jnp.where(first_half, GROUP // 2, 0), [one])
 
-            recv[piece, me] = send[piece, me]
 
     across = (jnp.where(mine > 0, GROUP, 0), jnp.minimum(mine, middle + 1) * GROUP)
 
@@ -296,6 +295,8 @@
             send_near(some)
             send_to(*across, some)
     send_to(mine * GROUP, me, everything)
+    for piece in everything:
+        recv[piece, me] = send[piece, me]
 
     @pl.when(low & first_half)
     def _():

time: 15.7 us -> 15.7 us (level)
  no operation moved by 1% of the time
where the time goes in v8:
time: 15.7 us; the launch traced here: 15.5 us
  Pallas kernels  15.4 us (98%)
    pallas_call x1, Pallas kernels, on_device(): pl.pallas_call(functools.partial(kernel, rows, cols, ('row', 'col')), out...  14.5 us
    pallas_call x1, Pallas kernels, on_device(): pl.pallas_call(last_kernel, out_shape=jax.ShapeDtypeStruct((fields, share...  0.91 us

profile of v8, /device:TPU:0, one launch (start us, length us, event | category | flops | bytes accessed | tf_op | source)
XLA Modules:
  0.0 15.5 jit_solution(6139377461299315241)
XLA Ops:
  0.0 0.0 copy-start
  0.0 14.5 %shard_map.73 = (f32[2,64,128]{2,1,0:T(8,128)S(1)}, f32[2,64,512]{2,1,0:T(8,128)S(1)}, f32[3,4,64,64]{3,2,1,0:T(8,128)S(1)}) custom-call(f32[2,8,32,128]{3,2,1,0:T(8,128)} %bitcast.4, bf16[256,256]{1,0:T(8,128)(2,1)} %constant.6.clone.hx_hbm, bf16[256,256]{1,0:T(8,128)(2,1)} %constant.7.clone.hy_hbm, bf16[2,256,512]{2,1,0:T(8,128)(2,1)} %constant.8.clone.wz_hbm.wz, ...), custom_call_target="tpu_custom_call" | custom-call | tf_op jit(solution)/shard_map/pallas_call | solution.py:411
  14.5 0.0 copy-done
  14.6 0.9 %shard_map.74 = f32[2,8,64,64]{3,2,1,0:T(8,128)} custom-call(f32[2,64,128]{2,1,0:T(8,128)S(1)} %get-tuple-element.8.lines, f32[2,64,512]{2,1,0:T(8,128)S(1)} %get-tuple-element.9.scale, f32[3,4,64,64]{3,2,1,0:T(8,128)S(1)} %get-tuple-element.10.early, bf16[2,256,512]{2,1,0:T(8,128)(2,1)S(1)} %copy-done), custom_call_target="tpu_custom_call" | custom-call | tf_op jit(solution)/shard_map/pallas_call | solution.py:446
Async XLA Ops:
  0.0 14.5 %copy-start = (bf16[2,256,512]{2,1,0:T(8,128)(2,1)S(1)}, bf16[2,256,512]{2,1,0:T(8,128)(2,1)}, u32[]{:S(2)}) copy-start(bf16[2,256,512]{2,1,0:T(8,128)(2,1)} %constant.8.clone.wz_hbm.wz) | copy-start | bytes 1572868

commit v9 on v7

--- a/solution.py
+++ b/solution.py
@@ -191,12 +191,13 @@
 
     def send_to(least, most, some):
         for piece in some:
-
-            def step(t, carry, piece=piece):
-                row_copy(piece, t).start()
-                return carry
-
-            lax.fori_loop(least, most, step, 0)
+            for parity in (0, 1):
+
+                def step(t, carry, piece=piece, parity=parity):
+                    row_copy(piece, least + 2 * t + parity).start()
+                    return carry
+
+                lax.fori_loop(0, (most - least + 1 - parity) // 2, step, 0)
 
     everything = range(pieces)
     front = jnp.minimum(mine, 1) * (GROUP // 2)

time: 15.7 us -> 15.8 us (level)
  no operation moved by 1% of the time
where the time goes in v9:
time: 15.8 us; the launch traced here: 15.5 us
  Pallas kernels  15.5 us (98%)
    pallas_call x1, Pallas kernels, on_device(): pl.pallas_call(functools.partial(kernel, rows, cols, ('row', 'col')), out...  14.6 us
    pallas_call x1, Pallas kernels, on_device(): pl.pallas_call(last_kernel, out_shape=jax.ShapeDtypeStruct((fields, share...  0.91 us

profile of v9, /device:TPU:0, one launch (start us, length us, event | category | flops | bytes accessed | tf_op | source)
XLA Modules:
  0.0 15.5 jit_solution(14289078368331801669)
XLA Ops:
  0.0 0.0 copy-start
  0.0 14.6 %shard_map.73 = (f32[2,64,128]{2,1,0:T(8,128)S(1)}, f32[2,64,512]{2,1,0:T(8,128)S(1)}, f32[3,4,64,64]{3,2,1,0:T(8,128)S(1)}) custom-call(f32[2,8,32,128]{3,2,1,0:T(8,128)} %bitcast.4, bf16[256,256]{1,0:T(8,128)(2,1)} %constant.6.clone.hx_hbm, bf16[256,256]{1,0:T(8,128)(2,1)} %constant.7.clone.hy_hbm, bf16[2,256,512]{2,1,0:T(8,128)(2,1)} %constant.8.clone.wz_hbm.wz, ...), custom_call_target="tpu_custom_call" | custom-call | tf_op jit(solution)/shard_map/pallas_call | solution.py:411
  14.6 0.0 copy-done
  14.6 0.9 %shard_map.74 = f32[2,8,64,64]{3,2,1,0:T(8,128)} custom-call(f32[2,64,128]{2,1,0:T(8,128)S(1)} %get-tuple-element.8.lines, f32[2,64,512]{2,1,0:T(8,128)S(1)} %get-tuple-element.9.scale, f32[3,4,64,64]{3,2,1,0:T(8,128)S(1)} %get-tuple-element.10.early, bf16[2,256,512]{2,1,0:T(8,128)(2,1)S(1)} %copy-done), custom_call_target="tpu_custom_call" | custom-call | tf_op jit(solution)/shard_map/pallas_call | solution.py:446
Async XLA Ops:
  0.0 14.6 %copy-start = (bf16[2,256,512]{2,1,0:T(8,128)(2,1)S(1)}, bf16[2,256,512]{2,1,0:T(8,128)(2,1)}, u32[]{:S(2)}) copy-start(bf16[2,256,512]{2,1,0:T(8,128)(2,1)} %constant.8.clone.wz_hbm.wz) | copy-start | bytes 1572868
